TPU v7x, 256 devices: a whole 4x4x8 slice. The times are simulated.
256 devices in a mesh: dp: 16 (over x_hi, z), param: 16 (over y, x_lo, core).
Axes of the slice: x: 4 (x_hi: 2, x_lo: 2; x = x_hi * 2 + x_lo), y: 4, z: 8, core: 2. Of those that a mesh axis runs over, the one named last changes fastest.
Arguments:
- ex_grads: bfloat16 [1536, 20480], P('dp', 'param'), may hold values from -6 to 6
- tgt_grads: bfloat16 [4096, 20480], P('dp', 'param'), may hold values from -6 to 6
- projection: bfloat16 [20480, 4096], P('param'), may hold values from -0.0390625 to 0.0390625
- example_weight: float32 [1536], P('param'), may hold values from 0.05 to 1
Outputs:
- scores: float32 [4096, 1536], P('dp', 'param')
All inputs are finite; a program needn't handle non-finite values.
Results may differ from a plain program's by a relative error of at most 0.0078.
Values may be sent and summed in bfloat16 or wider, within the bound.
A program may use at most 192 MiB of HBM per device.

v0:
```python
import math
import jax
import jax.numpy as jnp
from jax import lax
from jax.sharding import PartitionSpec as P

ridge_value = 0.5


def sent_to_all(x, axis):
    length = lax.axis_size(axis)
    return lax.all_to_all(jnp.broadcast_to(x[None], (length, *x.shape)), axis, 0, 0, tiled=True)


def in_order(parts, dim):
    parts = jnp.moveaxis(parts, 0, dim)
    lengths = parts.shape
    return parts.reshape(*lengths[:dim], lengths[dim] * lengths[dim + 1], *lengths[dim + 2 :])


def gather_directly(x, axis, dim):
    parts = sent_to_all(x, axis)
    return in_order(parts, dim)


def with_ridge(block, first_row):
    row_ids = lax.broadcasted_iota(jnp.int32, block.shape, 0) + first_row
    col_ids = lax.broadcasted_iota(jnp.int32, block.shape, 1)
    return block + jnp.where(row_ids == col_ids, ridge_value, 0.0).astype(jnp.float32)


def on_device(ex_grads, tgt_grads, projection, example_weight):
    ex_rows = ex_grads.shape[0]
    columns = projection.shape[1]
    param_total = lax.axis_size("param")
    param_pos = lax.axis_index("param")
    replica_pos = lax.axis_index("dp")
    stacked = jnp.concatenate([ex_grads, tgt_grads], axis=0)
    contract_rows = (((0,), (1,)), ((), ()))
    feature_block = lax.psum_scatter(
        lax.dot_general(projection, stacked, contract_rows, preferred_element_type=jnp.float32),
        "param",
        scatter_dimension=0,
        tiled=True,
    )
    local_features = feature_block.astype(jnp.bfloat16)
    example_part = local_features[:, :ex_rows]
    contract_first = (((0,), (0,)), ((), ()))
    partial_value = lax.dot_general(
        local_features,
        gather_directly(example_part, "dp", 1),
        contract_first,
        preferred_element_type=jnp.float32,
    )
    examples = partial_value.shape[1]
    summed = lax.psum(partial_value, "param")
    kernel_block = with_ridge(summed[:ex_rows] / columns, replica_pos * ex_rows)
    kernel = lax.all_gather(kernel_block, "dp", axis=0, tiled=True)
    cross_terms = summed[ex_rows:] / columns
    factor = jnp.linalg.cholesky(kernel)
    forward = jax.scipy.linalg.solve_triangular(factor, cross_terms.T, lower=True)
    solved = jax.scipy.linalg.solve_triangular(factor, forward, lower=True, trans=1)
    block_cols = examples // param_total
    chosen = lax.dynamic_slice_in_dim(solved.T, param_pos * block_cols, block_cols, 1)
    return chosen * math.sqrt(columns) * example_weight[None, :]


def solution(mesh):
    placed = (P("dp", "param"), P("dp", "param"), P("param", None), P("param"))
    return jax.shard_map(
        on_device, mesh=mesh, in_specs=placed, out_specs=P("dp", "param"), check_vma=False
    )
```

profile of v0, /device:TPU:1, one launch (start us, length us, event | category | flops | bytes accessed | tf_op | source)
XLA Modules:
  0.0 965.1 jit_solution(2935307158991540555)
XLA Ops:
  6.5 10.7 %convolution_bitcast_fusion = f32[4096,352]{0,1:T(8,128)} fusion(bf16[1280,4096]{1,0:T(8,128)(2,1)} %param.6, bf16[256,1280]{1,0:T(8,128)(2,1)} %param.5, bf16[96,1280]{1,0:T(8,128)(2,1)} %param.4), kind=kOutput, calls=%fused_computation.6 | convolution fusion | flops 3692789760 | bytes 17154048 | tf_op jit(solution)/shard_map/dot_general | solution.py:41
  17.3 79.7 %reduce-scatter.2.cloned.1.call-done = f32[256,352]{0,1:T(8,128)} async-done(((f32[4096,352]{0,1:T(8,128)}), f32[256,352]{0,1:T(8,128)}) %reduce-scatter.2.cloned.1.call-update) | async-done | bytes 360464 | tf_op jit(solution)/shard_map/reduce_scatter | solution.py:40
  98.1 27.1 %all_to_all.5 = bf16[16,256,96]{1,2,0:T(8,128)(2,1)S(1)} all-to-all(bf16[16,256,96]{1,2,0:T(8,128)(2,1)S(1)} %broadcast_in_dim.17), channel_id=1, replica_groups=mesh['dp'=16,'param'=16] {'dp'}, dimensions={0} | all-to-all | bytes 1572864 | tf_op jit(solution)/shard_map/all_to_all | solution.py:12
  127.1 130.4 %all-reduce.3.cloned.1.call-done = f32[352,1536]{1,0:T(8,128)} async-done(((f32[352,1536]{1,0:T(8,128)}), f32[352,1536]{1,0:T(8,128)}) %all-reduce.3.cloned.1.call-update) | async-done | bytes 2162704 | tf_op jit(solution)/shard_map/psum | solution.py:56
  261.1 144.9 %all-gather.2.cloned.1.call-done = f32[1536,1536]{1,0:T(8,128)} async-done(((f32[96,1536]{1,0:T(8,128)}), f32[1536,1536]{1,0:T(8,128)}) %all-gather.2.cloned.1.call-update) | async-done | bytes 9437200 | tf_op jit(solution)/shard_map/all_gather | solution.py:58
  406.0 10.1 %copy.10 = f32[1536,1536]{0,1:T(8,128)} copy(f32[1536,1536]{1,0:T(8,128)} %all-gather.2.cloned.1.call-done) | data formatting | bytes 18874368 | tf_op jit(solution)/shard_map/all_gather | solution.py:58
  416.1 12.3 %fusion = f32[1536,1536]{1,0:T(8,128)} fusion(f32[1536,1536]{1,0:T(8,128)} %all-gather.2.cloned.1.call-done, f32[1536,1536]{0,1:T(8,128)} %copy.10), kind=kLoop, calls=%fused_computation.4 | loop fusion | flops 4718592 | bytes 28311552 | tf_op jit(solution)/shard_map/jit(cholesky)/div | solution.py:60
  429.3 11.7 %cholesky.341 = f32[128,128]{1,0:T(8,128)S(1)} custom-call(f32[128,128]{1,0:T(8,128)S(1)} %cholesky.892), custom_call_target="Cholesky" | custom-call | tf_op jit(solution)/shard_map/jit(cholesky)/cholesky | solution.py:60
  441.0 4.8 cholesky.371
  445.8 9.8 %custom-call.98 = f32[1,128,128]{1,2,0:T(8,128)S(1)} custom-call(f32[1,128,128]{2,1,0:T(8,128)S(1)} %get-tuple-element.111), custom_call_target="InvertDiagBlocksLowerTriangular" | custom-call | tf_op jit(solution)/shard_map/jit(cholesky)/cholesky | solution.py:60
  455.6 2.8 constant_dynamic-update-slice_fusion.134
  460.3 11.9 %cholesky.362 = f32[128,128]{1,0:T(8,128)S(1)} custom-call(f32[128,128]{1,0:T(8,128)S(1)} %cholesky.896), custom_call_target="Cholesky" | custom-call | tf_op jit(solution)/shard_map/jit(cholesky)/cholesky | solution.py:60
  472.9 9.8 %custom-call.99 = f32[1,128,128]{1,2,0:T(8,128)S(1)} custom-call(f32[1,128,128]{2,1,0:T(8,128)S(1)} %get-tuple-element.108), custom_call_target="InvertDiagBlocksLowerTriangular" | custom-call | tf_op jit(solution)/shard_map/jit(cholesky)/cholesky | solution.py:60
  484.2 2.8 convolution_subtract_fusion.1
  487.0 11.7 %cholesky.385 = f32[128,128]{1,0:T(8,128)S(1)} custom-call(f32[128,128]{1,0:T(8,128)S(1)} %cholesky.901), custom_call_target="Cholesky" | custom-call | tf_op jit(solution)/shard_map/jit(cholesky)/cholesky | solution.py:60
  499.4 10.0 %custom-call.100 = f32[1,128,128]{1,2,0:T(8,128)S(1)} custom-call(f32[1,128,128]{2,1,0:T(8,128)S(1)} %get-tuple-element.105), custom_call_target="InvertDiagBlocksLowerTriangular" | custom-call | tf_op jit(solution)/shard_map/jit(cholesky)/cholesky | solution.py:60
  510.9 3.3 convolution_subtract_fusion
  514.3 11.7 %cholesky.715 = f32[128,128]{1,0:T(8,128)S(1)} custom-call(f32[128,128]{1,0:T(8,128)S(1)} %cholesky.906), custom_call_target="Cholesky" | custom-call | tf_op jit(solution)/shard_map/jit(cholesky)/cholesky | solution.py:60
  526.6 9.8 %custom-call.101 = f32[1,128,128]{1,2,0:T(8,128)S(1)} custom-call(f32[1,128,128]{2,1,0:T(8,128)S(1)} %get-tuple-element.102), custom_call_target="InvertDiagBlocksLowerTriangular" | custom-call | tf_op jit(solution)/shard_map/jit(cholesky)/cholesky | solution.py:60
  537.8 3.6 fusion.18
  541.4 12.1 %cholesky.734 = f32[128,128]{1,0:T(8,128)S(1)} custom-call(f32[128,128]{1,0:T(8,128)S(1)} %cholesky.911), custom_call_target="Cholesky" | custom-call | tf_op jit(solution)/shard_map/jit(cholesky)/cholesky | solution.py:60
  554.2 9.8 %custom-call.102 = f32[1,128,128]{1,2,0:T(8,128)S(1)} custom-call(f32[1,128,128]{2,1,0:T(8,128)S(1)} %get-tuple-element.99), custom_call_target="InvertDiagBlocksLowerTriangular" | custom-call | tf_op jit(solution)/shard_map/jit(cholesky)/cholesky | solution.py:60
  565.3 3.8 fusion.21
  569.1 11.7 %cholesky.754 = f32[128,128]{1,0:T(8,128)S(1)} custom-call(f32[128,128]{1,0:T(8,128)S(1)} %cholesky.916), custom_call_target="Cholesky" | custom-call | tf_op jit(solution)/shard_map/jit(cholesky)/cholesky | solution.py:60
  581.5 10.0 %custom-call.103 = f32[1,128,128]{1,2,0:T(8,128)S(1)} custom-call(f32[1,128,128]{2,1,0:T(8,128)S(1)} %get-tuple-element.96), custom_call_target="InvertDiagBlocksLowerTriangular" | custom-call | tf_op jit(solution)/shard_map/jit(cholesky)/cholesky | solution.py:60
  592.8 3.8 fusion.24
  596.6 11.7 %cholesky.774 = f32[128,128]{1,0:T(8,128)S(1)} custom-call(f32[128,128]{1,0:T(8,128)S(1)} %cholesky.921), custom_call_target="Cholesky" | custom-call | tf_op jit(solution)/shard_map/jit(cholesky)/cholesky | solution.py:60
  609.0 9.8 %custom-call.104 = f32[1,128,128]{1,2,0:T(8,128)S(1)} custom-call(f32[1,128,128]{2,1,0:T(8,128)S(1)} %get-tuple-element.93), custom_call_target="InvertDiagBlocksLowerTriangular" | custom-call | tf_op jit(solution)/shard_map/jit(cholesky)/cholesky | solution.py:60
  620.0 4.1 fusion.27
  624.1 11.7 %cholesky.794 = f32[128,128]{1,0:T(8,128)S(1)} custom-call(f32[128,128]{1,0:T(8,128)S(1)} %cholesky.926), custom_call_target="Cholesky" | custom-call | tf_op jit(solution)/shard_map/jit(cholesky)/cholesky | solution.py:60
  636.5 9.8 %custom-call.105 = f32[1,128,128]{1,2,0:T(8,128)S(1)} custom-call(f32[1,128,128]{2,1,0:T(8,128)S(1)} %get-tuple-element.90), custom_call_target="InvertDiagBlocksLowerTriangular" | custom-call | tf_op jit(solution)/shard_map/jit(cholesky)/cholesky | solution.py:60
  647.4 3.6 fusion.30
  650.9 12.2 %cholesky.814 = f32[128,128]{1,0:T(8,128)S(1)} custom-call(f32[128,128]{1,0:T(8,128)S(1)} %cholesky.931), custom_call_target="Cholesky" | custom-call | tf_op jit(solution)/shard_map/jit(cholesky)/cholesky | solution.py:60
  663.7 9.8 %custom-call.106 = f32[1,128,128]{1,2,0:T(8,128)S(1)} custom-call(f32[1,128,128]{2,1,0:T(8,128)S(1)} %get-tuple-element.87), custom_call_target="InvertDiagBlocksLowerTriangular" | custom-call | tf_op jit(solution)/shard_map/jit(cholesky)/cholesky | solution.py:60
  674.6 3.3 fusion.33
  677.9 11.7 %cholesky.834 = f32[128,128]{1,0:T(8,128)S(1)} custom-call(f32[128,128]{1,0:T(8,128)S(1)} %cholesky.936), custom_call_target="Cholesky" | custom-call | tf_op jit(solution)/shard_map/jit(cholesky)/cholesky | solution.py:60
  690.2 9.8 %custom-call.107 = f32[1,128,128]{1,2,0:T(8,128)S(1)} custom-call(f32[1,128,128]{2,1,0:T(8,128)S(1)} %get-tuple-element.84), custom_call_target="InvertDiagBlocksLowerTriangular" | custom-call | tf_op jit(solution)/shard_map/jit(cholesky)/cholesky | solution.py:60
  701.0 2.7 fusion.36
  703.7 11.9 %cholesky.854 = f32[128,128]{1,0:T(8,128)S(1)} custom-call(f32[128,128]{1,0:T(8,128)S(1)} %cholesky.941), custom_call_target="Cholesky" | custom-call | tf_op jit(solution)/shard_map/jit(cholesky)/cholesky | solution.py:60
  716.2 9.8 %custom-call.108 = f32[1,128,128]{1,2,0:T(8,128)S(1)} custom-call(f32[1,128,128]{2,1,0:T(8,128)S(1)} %get-tuple-element.81), custom_call_target="InvertDiagBlocksLowerTriangular" | custom-call | tf_op jit(solution)/shard_map/jit(cholesky)/cholesky | solution.py:60
  726.9 2.3 convolution_subtract_fusion.25
  729.2 11.7 %cholesky.872 = f32[128,128]{1,0:T(8,128)S(1)} custom-call(f32[128,128]{1,0:T(8,128)S(1)} %convolution_subtract_fusion.25), custom_call_target="Cholesky" | custom-call | tf_op jit(solution)/shard_map/jit(cholesky)/cholesky | solution.py:60
  756.7 8.5 select_select_fusion
  765.2 35.2 %while.1 = (s32[]{:T(128)}, f32[1536,1536]{1,0:T(8,128)}, s32[12,2]{0,1:T(2,128)S(1)}, f32[12,128,128]{2,1,0:T(8,128)S(1)}, s32[]{:T(128)}) while((s32[]{:T(128)}, f32[1536,1536]{1,0:T(8,128)}, s32[12,2]{0,1:T(2,128)S(1)}, f32[12,128,128]{2,1,0:T(8,128)S(1)}, s32[]{:T(128)}) %tuple.106), condition=%wide.while_cond, body=%wide.while_body.sunk | while | flops 2 | bytes 131189 | solution.py:62
  765.9 2.2 bitcast_dynamic-update-slice_fusion.2
  768.8 2.2 bitcast_dynamic-update-slice_fusion.2
  800.4 118.3 %custom-call.109 = f32[12,128,128]{1,2,0:T(8,128)S(1)} custom-call(f32[12,128,128]{2,1,0:T(8,128)S(1)} %get-tuple-element.12), custom_call_target="InvertDiagBlocksLowerTriangular" | custom-call | tf_op jit(solution)/shard_map/jit(_solve_triangular)/triangular_solve | solution.py:62
  941.0 2.4 convolution_subtract_fusion.24
  (206 shorter events, 103.2 us)
Async XLA Ops:
  6.5 90.4 %reduce-scatter.2.cloned.1.call-start = ((), (), s32[]{:S(2)}) async-start(), calls=%async_computation.2 | async-start | bytes 6127616 | tf_op jit(solution)/shard_map/reduce_scatter | solution.py:40
  17.2 240.3 %all-reduce.3.cloned.1.call-start = ((), (), s32[]{:S(2)}) async-start(), calls=%async_computation.3 | async-start | bytes 4325376 | tf_op jit(solution)/shard_map/psum | solution.py:56
  127.0 132.5 %copy-start.1 = (f32[96]{0:T(128)S(1)}, f32[96]{0:T(128)}, u32[]{:S(2)}) copy-start(f32[96]{0:T(128)} %param.7) | copy-start | bytes 1156
  127.1 278.9 %all-gather.2.cloned.1.call-start = ((), (), s32[]{:S(2)}) async-start(), calls=%async_computation.4 | async-start | bytes 10027008 | tf_op jit(solution)/shard_map/all_gather | solution.py:58
  920.3 9.7 %copy-start = (f32[1536,1536]{1,0:T(8,128)S(1)}, f32[1536,1536]{1,0:T(8,128)}, u32[]{:S(2)}) copy-start(f32[1536,1536]{1,0:T(8,128)} %get-tuple-element.190) | copy-start | bytes 28311556
Sparse Core Ops, SparseCore 0:
  17.4 79.5 reduce-scatter.1
  127.2 130.2 all-reduce.2
  260.1 145.8 all-gather.1
where the time goes:
time: 970 us; the launch traced here: 965 us
  other arithmetic  409 us (42%)
  waiting for transfers between devices  355 us (37%)
  matrix products  100 us (10%)
  local copies, waits for them, and re-layouts  51.6 us (5%)
  blocking collectives  27.1 us (3%)
  between operations  22.1 us (2%)
    another operation x46, other arithmetic, on_device(): factor = jnp.linalg.cholesky(kernel)  265 us
    all_gather x1, waiting for transfers between devices, on_device(): kernel = lax.all_gather(kernel_block, 'dp', axis=0, tiled=True)  145 us
    psum x1, waiting for transfers between devices, on_device(): summed = lax.psum(partial_value, 'param')  130 us
    another operation x3, other arithmetic, on_device(): jax.scipy.linalg.solve_triangular(factor, forward, lower=True, trans=1)  127 us
    reduce_scatter x1, waiting for transfers between devices, on_device(): lax.psum_scatter(lax.dot_general(projection, stacked, contract_rows, pref...  79.7 us
    another operation x22, matrix products, on_device(): factor = jnp.linalg.cholesky(kernel)  50.1 us
    another operation x36, local copies, waits for them, and re-layouts  35 us
    all_to_all x1, blocking collectives, sent_to_all(): lax.all_to_all(jnp.broadcast_to(x[None], (length, *x.shape)), axis, 0, 0,...  27.1 us
  transfers between devices with their start and end apart: 3, of which 3 were waited for; matrix products, arithmetic and copies ran while one was open for 0% of the time, Pallas kernels for 0%

commit v1 on v0

--- a/solution.py
+++ b/solution.py
@@ -53,7 +53,8 @@
         preferred_element_type=jnp.float32,
     )
     examples = partial_value.shape[1]
-    summed = lax.psum(partial_value, "param")
+    pieces = lax.all_gather(partial_value, "param")
+    summed = jnp.sum(pieces, axis=0)
     kernel_block = with_ridge(summed[:ex_rows] / columns, replica_pos * ex_rows)
     kernel = lax.all_gather(kernel_block, "dp", axis=0, tiled=True)
     cross_terms = summed[ex_rows:] / columns

time: 970 us -> 1030 us (1.062)
  waiting for transfers between devices: 355 us -> 401 us
  other arithmetic: 409 us -> 420 us
  local copies, waits for them, and re-layouts: 51.6 us -> 62.5 us
    all_gather x0 -> x1, waiting for transfers between devices: none -> 179 us  [on_device(): pieces = lax.all_gather(partial_value, 'param')]
    psum x1 -> x0, waiting for transfers between devices: 130 us -> none  [on_device(): summed = lax.psum(partial_value, 'param')]
    reduce_sum x0 -> x1, other arithmetic: none -> 12.2 us  [on_device(): summed = jnp.sum(pieces, axis=0)]
where the time goes in v1:
time: 1030 us; the launch traced here: 1020 us
  other arithmetic  420 us (41%)
  waiting for transfers between devices  401 us (39%)
  matrix products  90.6 us (9%)
  local copies, waits for them, and re-layouts  62.5 us (6%)
  blocking collectives  26.7 us (3%)
  between operations  22.3 us (2%)
    another operation x46, other arithmetic, on_device(): factor = jnp.linalg.cholesky(kernel)  265 us
    all_gather x1, waiting for transfers between devices, on_device(): pieces = lax.all_gather(partial_value, 'param')  179 us
    all_gather x1, waiting for transfers between devices, on_device(): kernel = lax.all_gather(kernel_block, 'dp', axis=0, tiled=True)  142 us
    another operation x3, other arithmetic, on_device(): jax.scipy.linalg.solve_triangular(factor, forward, lower=True, trans=1)  127 us
    reduce_scatter x1, waiting for transfers between devices, on_device(): lax.psum_scatter(lax.dot_general(projection, stacked, contract_rows, pref...  79.7 us
    another operation x22, matrix products, on_device(): factor = jnp.linalg.cholesky(kernel)  50.3 us
    another operation x36, local copies, waits for them, and re-layouts  42.9 us
    all_to_all x1, blocking collectives, sent_to_all(): lax.all_to_all(jnp.broadcast_to(x[None], (length, *x.shape)), axis, 0, 0,...  26.7 us
  transfers between devices with their start and end apart: 3, of which 3 were waited for; matrix products, arithmetic and copies ran while one was open for 0% of the time, Pallas kernels for 0%

profile of v1, /device:TPU:1, one launch (start us, length us, event | category | flops | bytes accessed | tf_op | source)
XLA Modules:
  0.0 1022.5 jit_solution(11903064251099431684)
XLA Ops:
  6.5 10.7 %convolution_bitcast_fusion = f32[4096,352]{0,1:T(8,128)} fusion(bf16[1280,4096]{1,0:T(8,128)(2,1)} %param.6, bf16[256,1280]{1,0:T(8,128)(2,1)} %param.5, bf16[96,1280]{1,0:T(8,128)(2,1)} %param.4), kind=kOutput, calls=%fused_computation.6 | convolution fusion | flops 3692789760 | bytes 17154048 | tf_op jit(solution)/shard_map/dot_general | solution.py:41
  17.3 79.7 %reduce-scatter.2.cloned.1.call-done = f32[256,352]{0,1:T(8,128)} async-done(((f32[4096,352]{0,1:T(8,128)}), f32[256,352]{0,1:T(8,128)}) %reduce-scatter.2.cloned.1.call-update) | async-done | bytes 360464 | tf_op jit(solution)/shard_map/reduce_scatter | solution.py:40
  98.1 26.7 %all_to_all.5 = bf16[16,256,96]{1,2,0:T(8,128)(2,1)S(1)} all-to-all(bf16[16,256,96]{1,2,0:T(8,128)(2,1)S(1)} %broadcast_in_dim.17), channel_id=1, replica_groups=mesh['dp'=16,'param'=16] {'dp'}, dimensions={0} | all-to-all | bytes 1572864 | tf_op jit(solution)/shard_map/all_to_all | solution.py:12
  126.7 178.8 %all-gather.6.cloned.1.call-done = f32[5632,1536]{1,0:T(8,128)} async-done(((f32[352,1536]{1,0:T(8,128)}), f32[5632,1536]{1,0:T(8,128)}) %all-gather.6.cloned.1.call-update) | async-done | bytes 34603024 | tf_op jit(solution)/shard_map/all_gather | solution.py:56
  305.5 12.2 %reduce_sum.9 = f32[352,1536]{1,0:T(8,128)S(1)} reduce(f32[16,352,1536]{2,1,0:T(8,128)} %bitcast.208, f32[]{:T(128)} %constant.418.clone.1), dimensions={0}, to_apply=%region_1.0 | reduce | flops 8110080 | bytes 36765700 | tf_op jit(solution)/shard_map/reduce_sum | solution.py:57
  322.0 142.4 %all-gather.4.cloned.1.call-done = f32[1536,1536]{1,0:T(8,128)} async-done(((f32[96,1536]{1,0:T(8,128)}), f32[1536,1536]{1,0:T(8,128)}) %all-gather.4.cloned.1.call-update) | async-done | bytes 9437200 | tf_op jit(solution)/shard_map/all_gather | solution.py:59
  464.3 9.9 copy.8
  474.2 12.6 %fusion = f32[1536,1536]{1,0:T(8,128)} fusion(f32[1536,1536]{1,0:T(8,128)} %all-gather.4.cloned.1.call-done, f32[1536,1536]{0,1:T(8,128)} %copy.8), kind=kLoop, calls=%fused_computation.4 | loop fusion | flops 4718592 | bytes 28311552 | tf_op jit(solution)/shard_map/jit(cholesky)/div | solution.py:61
  487.6 11.7 %cholesky.341 = f32[128,128]{1,0:T(8,128)S(1)} custom-call(f32[128,128]{1,0:T(8,128)S(1)} %cholesky.892), custom_call_target="Cholesky" | custom-call | tf_op jit(solution)/shard_map/jit(cholesky)/cholesky | solution.py:61
  499.4 4.9 cholesky.371
  504.2 9.8 custom-call.98
  518.7 12.1 %cholesky.362 = f32[128,128]{1,0:T(8,128)S(1)} custom-call(f32[128,128]{1,0:T(8,128)S(1)} %cholesky.896), custom_call_target="Cholesky" | custom-call | tf_op jit(solution)/shard_map/jit(cholesky)/cholesky | solution.py:61
  531.4 9.8 custom-call.99
  545.6 11.7 %cholesky.385 = f32[128,128]{1,0:T(8,128)S(1)} custom-call(f32[128,128]{1,0:T(8,128)S(1)} %cholesky.901), custom_call_target="Cholesky" | custom-call | tf_op jit(solution)/shard_map/jit(cholesky)/cholesky | solution.py:61
  558.7 10.0 custom-call.100
  570.1 3.3 convolution_subtract_fusion
  573.5 11.7 %cholesky.715 = f32[128,128]{1,0:T(8,128)S(1)} custom-call(f32[128,128]{1,0:T(8,128)S(1)} %cholesky.906), custom_call_target="Cholesky" | custom-call | tf_op jit(solution)/shard_map/jit(cholesky)/cholesky | solution.py:61
  586.5 9.8 custom-call.101
  597.8 3.7 fusion.17
  601.5 11.9 %cholesky.734 = f32[128,128]{1,0:T(8,128)S(1)} custom-call(f32[128,128]{1,0:T(8,128)S(1)} %cholesky.911), custom_call_target="Cholesky" | custom-call | tf_op jit(solution)/shard_map/jit(cholesky)/cholesky | solution.py:61
  614.7 9.8 custom-call.102
  625.9 3.8 fusion.20
  629.7 11.7 %cholesky.754 = f32[128,128]{1,0:T(8,128)S(1)} custom-call(f32[128,128]{1,0:T(8,128)S(1)} %cholesky.916), custom_call_target="Cholesky" | custom-call | tf_op jit(solution)/shard_map/jit(cholesky)/cholesky | solution.py:61
  642.8 10.2 custom-call.103
  654.2 3.8 fusion.23
  658.1 11.7 %cholesky.774 = f32[128,128]{1,0:T(8,128)S(1)} custom-call(f32[128,128]{1,0:T(8,128)S(1)} %cholesky.921), custom_call_target="Cholesky" | custom-call | tf_op jit(solution)/shard_map/jit(cholesky)/cholesky | solution.py:61
  671.1 9.8 custom-call.104
  682.1 4.0 fusion.26
  686.1 11.7 %cholesky.794 = f32[128,128]{1,0:T(8,128)S(1)} custom-call(f32[128,128]{1,0:T(8,128)S(1)} %cholesky.926), custom_call_target="Cholesky" | custom-call | tf_op jit(solution)/shard_map/jit(cholesky)/cholesky | solution.py:61
  699.1 9.8 custom-call.105
  710.1 3.6 fusion.29
  713.6 12.1 %cholesky.814 = f32[128,128]{1,0:T(8,128)S(1)} custom-call(f32[128,128]{1,0:T(8,128)S(1)} %cholesky.931), custom_call_target="Cholesky" | custom-call | tf_op jit(solution)/shard_map/jit(cholesky)/cholesky | solution.py:61
  727.0 9.8 custom-call.106
  737.8 3.3 fusion.32
  741.2 11.7 %cholesky.834 = f32[128,128]{1,0:T(8,128)S(1)} custom-call(f32[128,128]{1,0:T(8,128)S(1)} %cholesky.936), custom_call_target="Cholesky" | custom-call | tf_op jit(solution)/shard_map/jit(cholesky)/cholesky | solution.py:61
  754.2 9.8 custom-call.107
  767.8 11.9 %cholesky.854 = f32[128,128]{1,0:T(8,128)S(1)} custom-call(f32[128,128]{1,0:T(8,128)S(1)} %cholesky.941), custom_call_target="Cholesky" | custom-call | tf_op jit(solution)/shard_map/jit(cholesky)/cholesky | solution.py:61
  781.0 9.8 custom-call.108
  793.9 11.7 %cholesky.872 = f32[128,128]{1,0:T(8,128)S(1)} custom-call(f32[128,128]{1,0:T(8,128)S(1)} %convolution_subtract_fusion.25), custom_call_target="Cholesky" | custom-call | tf_op jit(solution)/shard_map/jit(cholesky)/cholesky | solution.py:61
  815.2 8.5 select_select_fusion
  823.7 42.9 %while.1 = (s32[]{:T(128)}, f32[1536,1536]{1,0:T(8,128)}, s32[12,2]{0,1:T(2,128)S(1)}, f32[12,128,128]{2,1,0:T(8,128)}, s32[]{:T(128)}) while((s32[]{:T(128)}, f32[1536,1536]{1,0:T(8,128)}, s32[12,2]{0,1:T(2,128)S(1)}, f32[12,128,128]{2,1,0:T(8,128)}, s32[]{:T(128)}) %tuple.106), condition=%wide.while_cond, body=%wide.while_body.sunk | while | flops 2 | bytes 132705 | solution.py:63
  824.3 2.9 bitcast_dynamic-update-slice_fusion.2
  831.5 2.9 bitcast_dynamic-update-slice_fusion.2
  835.1 2.9 bitcast_dynamic-update-slice_fusion.2
  842.2 2.9 bitcast_dynamic-update-slice_fusion.2
  856.6 2.9 bitcast_dynamic-update-slice_fusion.2
  860.1 2.9 bitcast_dynamic-update-slice_fusion.2
  866.6 118.9 %custom-call.109 = f32[12,128,128]{1,2,0:T(8,128)S(1)} custom-call(f32[12,128,128]{2,1,0:T(8,128)} %get-tuple-element.12), custom_call_target="InvertDiagBlocksLowerTriangular" | custom-call | tf_op jit(solution)/shard_map/jit(_solve_triangular)/triangular_solve | solution.py:63
  (209 shorter events, 102.2 us)
Async XLA Ops:
  6.5 90.4 %reduce-scatter.2.cloned.1.call-start = ((), (), s32[]{:S(2)}) async-start(), calls=%async_computation.2 | async-start | bytes 6127616 | tf_op jit(solution)/shard_map/reduce_scatter | solution.py:40
  17.2 288.2 %all-gather.6.cloned.1.call-start = ((), (), s32[]{:S(2)}) async-start(), calls=%async_computation.4 | async-start | bytes 36765696 | tf_op jit(solution)/shard_map/all_gather | solution.py:56
  126.6 337.7 %all-gather.4.cloned.1.call-start = ((), (), s32[]{:S(2)}) async-start(), calls=%async_computation.3 | async-start | bytes 10027008 | tf_op jit(solution)/shard_map/all_gather | solution.py:59
  317.6 1.0 copy-start.1
  986.9 7.9 copy-start
Sparse Core Ops, SparseCore 0:
  17.4 79.5 reduce-scatter.1
  126.7 178.6 all-gather.5
  318.8 145.5 all-gather.3
